TPU v7x, 512 devices: a whole 4x8x8 slice. The times are simulated.
512 devices in a mesh: row: 16 (over z_lo, y), col: 32 (over x, z_hi, core).
Axes of the slice: x: 4, y: 8, z: 8 (z_hi: 4, z_lo: 2; z = z_hi * 2 + z_lo), core: 2. Of those that a mesh axis runs over, the one named last changes fastest.
Arguments:
- amplitudes: bfloat16 [4096, 262144], P(None, ('row', 'col')), may hold values from -6 to 6
- integrals: bfloat16 [256, 262144], P(None, ('row', 'col')), may hold values from -6 to 6
- hh_coupling: bfloat16 [256, 4096], P('row'), may hold values from -0.09375 to 0.09375
- thc_factor: bfloat16 [512, 1024], P(None, ('row', 'col')), may hold values from -0.25 to 0.25
- thc_core: float32 [1024, 1024], P('col', 'row'), may hold values from -3 to 3
- occ_energy: float32 [64], replicated, may hold values from -2 to -0.5
- vir_energy: float32 [512], replicated, may hold values from 0.3 to 3
- pair_owner: int32 [256], replicated, may hold values from 0 to 4095, as said below
Outputs:
- updated: bfloat16 [256, 262144], P(None, ('row', 'col'))
Inputs may be any that keep to these rules, and one draw needn't show every extreme that they name: pair_owner holds 256 distinct occupied pairs.
All inputs are finite; a program needn't handle non-finite values.
Results may differ from a plain program's by a relative error of at most 0.007.
Values may be sent and summed in bfloat16 or wider, within the bound.
A program may use at most 64 MiB of HBM per device.

v0:
```python
import jax
import jax.numpy as jnp
from jax import lax
from jax.sharding import Mesh
from jax.sharding import PartitionSpec as P

ROW = ("row_0", "row_1")
ROW_COL = ("row_0", "row_1", "col")


def in_order(pieces, dim):
    pieces = jnp.moveaxis(pieces, 0, dim)
    dims = pieces.shape
    return pieces.reshape(*dims[:dim], dims[dim] * dims[dim + 1], *dims[dim + 2 :])


def sent_to_all(shard, axis):
    count = lax.axis_size(axis)
    return lax.all_to_all(
        jnp.broadcast_to(shard[None], (count, *shard.shape)), axis, 0, 0, tiled=True
    )


def gather_directly(shard, axis, dim):
    return in_order(sent_to_all(shard, axis), dim)


def gather_in_order(shard, axes, order):
    pieces = shard[None]
    for k in order:
        pieces = lax.all_gather(pieces, axes[k], axis=0, tiled=True)
    carried = [lax.axis_size(axes[k]) for k in reversed(order)]
    pieces = pieces.reshape(*carried, *shard.shape)
    turned = sorted(range(len(order)), key=lambda place: order[len(order) - 1 - place])
    return pieces.transpose(*turned, *range(len(order), pieces.ndim)).reshape(-1, *shard.shape)


def gathered_by_axis(shard, axes, order, dim):
    return in_order(gather_in_order(shard, axes, order), dim)


def cut_along(shard, dim, count):
    dims = shard.shape
    pieces = shard.reshape(*dims[:dim], count, dims[dim] // count, *dims[dim + 1 :])
    return jnp.moveaxis(pieces, dim, 0)


def exchange_both(shard, axis, axes, splits, concats):
    sizes = [lax.axis_size(a) for a in axes]
    pieces = cut_along(shard, splits[0], sizes[0])
    pieces = jnp.moveaxis(cut_along(pieces, splits[1] + 1, sizes[1]), 0, 1)
    inside = pieces.shape[2:]
    pieces = pieces.reshape(-1, *inside)
    pieces = lax.all_to_all(pieces, axis, split_axis=0, concat_axis=0, tiled=True)
    pieces = in_order(pieces.reshape(*sizes, *inside), concats[0] + 1)
    return in_order(pieces, concats[1])


def per_device(
    amplitudes, integrals, hh_coupling, thc_factor, thc_core, occ_energy, vir_energy, pair_owner
):
    row_count = lax.axis_size(ROW)
    col_count = lax.axis_size("col")
    row_index = lax.axis_index(ROW)
    col_index = lax.axis_index("col")
    virtual = vir_energy.shape[0]
    column_width = amplitudes.shape[1]
    orb_block = column_width // virtual
    pairs_all = pair_owner.shape[0]
    pairs_col = pairs_all // col_count
    occupied = occ_energy.shape[0]
    factor = lax.all_gather(thc_factor, ROW_COL, axis=1, tiled=True)
    points = factor.shape[1]
    block_points = points // row_count
    core_block = gather_directly(thc_core, "col", 0)
    owned = amplitudes[pair_owner]
    coupled = jnp.dot(
        gathered_by_axis(hh_coupling, ROW, (0, 1), 0),
        amplitudes,
        preferred_element_type=jnp.float32,
    )
    local_half = jnp.einsum(
        "pkd,dq->pkq",
        owned.reshape(pairs_all, orb_block, virtual),
        factor,
        preferred_element_type=jnp.float32,
    ).astype(jnp.bfloat16)
    sectioned = local_half.reshape(col_count, pairs_col, 1, 1, orb_block, row_count, block_points)
    moved = exchange_both(sectioned, ROW_COL, (ROW, "col"), (5, 0), (2, 3))
    half = moved.reshape(pairs_col, virtual, block_points)
    middle = jnp.einsum("cP,pcq->pPq", factor, half, preferred_element_type=jnp.float32)
    weighted = (core_block[None] * middle).astype(jnp.bfloat16)
    back = jnp.einsum("aP,pPq->paq", factor, weighted, preferred_element_type=jnp.float32).astype(
        jnp.bfloat16
    )
    vir_slice = virtual // row_count
    sectioned_back = back.reshape(pairs_col, row_count, vir_slice, block_points)
    gathered_back = lax.all_to_all(sectioned_back, ROW, split_axis=1, concat_axis=3, tiled=True)
    gathered_back = gathered_back.reshape(pairs_col, vir_slice, row_count, block_points)
    factor_split = factor.reshape(virtual, row_count, block_points)
    partial_value = jnp.einsum(
        "parq,brq->rapb", gathered_back, factor_split, preferred_element_type=jnp.float32
    ).astype(jnp.bfloat16)
    ladder = jnp.sum(partial_value.astype(jnp.float32), axis=0).astype(jnp.bfloat16)
    ladder = ladder.reshape(col_count, orb_block, pairs_col, virtual)
    returned = lax.all_to_all(ladder, "col", split_axis=0, concat_axis=2, tiled=True)
    returned = (
        returned.reshape(orb_block, pairs_all, virtual)
        .transpose(1, 0, 2)
        .reshape(pairs_all, column_width)
    )
    device = row_index * col_count + col_index
    vir_mine = lax.dynamic_slice_in_dim(vir_energy, device * orb_block, orb_block, 0)
    orbital_ids = jnp.arange(occupied, dtype=jnp.int32)
    first_hit = (pair_owner // occupied)[:, None] == orbital_ids[None, :]
    second_hit = (pair_owner % occupied)[:, None] == orbital_ids[None, :]
    first_occ = jnp.sum(jnp.where(first_hit, occ_energy[None, :], 0.0), axis=1)
    second_occ = jnp.sum(jnp.where(second_hit, occ_energy[None, :], 0.0), axis=1)
    vir_pairs = vir_mine[:, None] + vir_energy[None, :]
    denom = vir_pairs - (first_occ + second_occ)[:, None]
    rest = integrals.astype(jnp.float32) + coupled + returned.astype(jnp.float32)
    update = 0.4 * owned.astype(jnp.float32) + 0.6 * rest / denom
    return update.astype(jnp.bfloat16)


def solution(mesh):
    finer = Mesh(mesh.devices.reshape(2, 8, mesh.shape["col"]), ("row_0", "row_1", "col"))
    in_specs = (
        P(None, ROW_COL),
        P(None, ROW_COL),
        P(ROW, None),
        P(None, ROW_COL),
        P("col", ROW),
        P(),
        P(),
        P(),
    )
    out_specs = P(None, ROW_COL)
    return jax.shard_map(
        per_device, mesh=finer, in_specs=in_specs, out_specs=out_specs, check_vma=False
    )
```

profile of v0, /device:TPU:1, one launch (start us, length us, event | category | flops | bytes accessed | tf_op | source)
XLA Modules:
  0.0 883.5 jit_solution(17219511499074198008)
XLA Ops:
  6.5 0.0 copy-start.3
  6.5 0.0 all-gather.7.cloned.1.call-start
  6.5 0.7 all-gather.7.cloned.1.call-update
  7.3 0.8 broadcast_in_dim.39
  8.0 1.0 reshape.74
  9.1 14.5 %all-to-all-start = ((f32[32,1,2048]{2,1,0:T(1,128)}), f32[32,1,2048]{2,1,0:T(1,128)}, u32[]{:S(2)}, u32[]{:S(2)}) async-start(f32[32,1,2048]{2,1,0:T(1,128)} %reshape.74), calls=%async_computation | async-start | bytes 524288 | tf_op jit(solution)/shard_map/all_to_all | solution.py:19
  23.5 0.0 all-gather.5.cloned.1.call-start
  23.6 10.7 %all-gather = bf16[32,4096]{1,0:T(8,128)(2,1)} all-gather(bf16[16,4096]{1,0:T(8,128)(2,1)} %param.10), channel_id=2, replica_groups=mesh['row_0'=2,'row_1'=8,'col'=32] {'row_0'}, dimensions={0}, use_global_device_ids=true | all-gather | bytes 393216 | tf_op jit(solution)/shard_map/all_gather | solution.py:31
  34.3 0.0 all-gather.5.cloned.1.call-update
  34.3 0.0 copy-done.3
  34.4 3.9 gather_fusion
  38.3 741.5 %all-gather.7.cloned.1.call-done = bf16[512,2,512]{2,1,0:T(2,128)(2,1)} async-done(((bf16[1,2,512]{2,1,0:T(2,128)(2,1)}), bf16[512,2,512]{2,1,0:T(2,128)(2,1)}) %all-gather.7.cloned.1.call-update) | async-done | bytes 1048592 | tf_op jit(solution)/shard_map/all_gather | solution.py:72
  779.8 1.5 reshape.68
  781.3 0.5 convolution_convert_fusion
  781.8 0.7 reshape_reshape.13
  782.4 0.3 copy.39
  782.7 0.0 copy-start
  782.7 1.4 reshape.72
  784.2 0.0 all-to-all-done
  784.2 12.4 %all-to-all-start.1 = ((bf16[512,2,256]{2,1,0:T(2,128)(2,1)}), bf16[512,2,256]{2,1,0:T(2,128)(2,1)S(1)}, u32[]{:S(2)}, u32[]{:S(2)}) async-start(bf16[512,2,256]{2,1,0:T(2,128)(2,1)} %reshape.72), calls=%async_computation.1 | async-start | bytes 1048576 | tf_op jit(solution)/shard_map/all_to_all | solution.py:54
  796.6 0.5 broadcast.20
  797.1 2.9 reduce.2
  800.0 1.1 reshape.75
  801.2 0.9 copy.38
  802.1 0.0 copy-done
  802.1 1.2 reshape.69
  803.3 20.9 %all-to-all-done.1 = bf16[512,2,256]{2,1,0:T(2,128)(2,1)S(1)} async-done(((bf16[512,2,256]{2,1,0:T(2,128)(2,1)}), bf16[512,2,256]{2,1,0:T(2,128)(2,1)S(1)}, u32[]{:S(2)}, u32[]{:S(2)}) %all-to-all-start.1) | async-done | bytes 524320 | tf_op jit(solution)/shard_map/all_to_all | solution.py:54
  824.2 0.6 reshape.73
  824.8 0.0 copy-start.1
  824.8 1.0 bitcast_bitcast_fusion
  825.9 0.5 copy-done.1
  826.4 4.2 fusion.1
  830.6 1.5 copy.43
  832.1 0.1 copy.55
  832.2 0.7 reshape.76
  833.0 15.6 %all_to_all.34 = bf16[16,2,8192]{2,1,0:T(2,128)(2,1)S(1)} all-to-all(bf16[16,2,8192]{2,1,0:T(2,128)(2,1)S(1)} %reshape.76), channel_id=1, replica_groups=mesh['row_0'=2,'row_1'=8,'col'=32] {'row_0','row_1'}, dimensions={0} | all-to-all | bytes 1048576 | tf_op jit(solution)/shard_map/all_to_all | solution.py:98
  848.5 0.7 reshape.77
  849.2 0.0 copy-start.2
  849.2 0.0 copy-start.4
  849.2 1.2 convert_reduce_fusion
  850.4 0.9 copy.45
  851.3 7.9 all-to-all-start.3
  859.2 0.0 copy-done.2
  859.2 0.7 dynamic_slice.3
  859.9 0.0 copy-done.4
  859.9 0.1 select_reduce_fusion
  860.0 0.6 broadcast_add_fusion
  860.6 0.0 all-gather.5.cloned.1.call-done
  860.7 0.0 copy-start.5
  860.7 1.8 copy.37
  862.4 10.0 %all-to-all-done.3 = bf16[32,1,8,512]{3,2,1,0:T(8,128)(2,1)S(1)} async-done(((bf16[32,1,8,512]{3,2,1,0:T(8,128)(2,1)}), bf16[32,1,8,512]{3,2,1,0:T(8,128)(2,1)S(1)}, u32[]{:S(2)}, u32[]{:S(2)}) %all-to-all-start.3) | async-done | bytes 262176 | tf_op jit(solution)/shard_map/all_to_all | solution.py:106
  872.5 0.0 copy-done.5
  872.5 4.2 fusion.6
  (3 shorter events, 0.0 us)
Async XLA Ops:
  6.5 27.8 %copy-start.3 = (s32[256]{0:T(256)S(1)}, s32[256]{0:T(256)}, u32[]{:S(2)}) copy-start(s32[256]{0:T(256)} %param.15) | copy-start | bytes 3076
  6.5 773.3 %all-gather.7.cloned.1.call-start = ((), (), s32[]{:S(2)}) async-start(), calls=%async_computation.5 | async-start | bytes 1050624 | tf_op jit(solution)/shard_map/all_gather | solution.py:72
  9.1 775.1 %all-to-all-start = ((f32[32,1,2048]{2,1,0:T(1,128)}), f32[32,1,2048]{2,1,0:T(1,128)}, u32[]{:S(2)}, u32[]{:S(2)}) async-start(f32[32,1,2048]{2,1,0:T(1,128)} %reshape.74), calls=%async_computation | async-start | bytes 524288 | tf_op jit(solution)/shard_map/all_to_all | solution.py:19
  23.5 837.1 %all-gather.5.cloned.1.call-start = ((), (), s32[]{:S(2)}) async-start(), calls=%async_computation.4 | async-start | bytes 2359296 | tf_op jit(solution)/shard_map/all_gather | solution.py:31
  782.7 19.4 %copy-start = (bf16[512,2,512]{2,1,0:T(2,128)(2,1)S(1)}, bf16[512,2,512]{2,1,0:T(2,128)(2,1)}, u32[]{:S(2)}) copy-start(bf16[512,2,512]{2,1,0:T(2,128)(2,1)} %all-gather.7.cloned.1.call-done) | copy-start | bytes 3145732
  784.2 40.0 %all-to-all-start.1 = ((bf16[512,2,256]{2,1,0:T(2,128)(2,1)}), bf16[512,2,256]{2,1,0:T(2,128)(2,1)S(1)}, u32[]{:S(2)}, u32[]{:S(2)}) async-start(bf16[512,2,256]{2,1,0:T(2,128)(2,1)} %reshape.72), calls=%async_computation.1 | async-start | bytes 1048576 | tf_op jit(solution)/shard_map/all_to_all | solution.py:54
  824.8 1.6 copy-start.1
  849.2 10.0 %copy-start.2 = (f32[512]{0:T(512)S(1)}, f32[512]{0:T(512)}, u32[]{:S(2)}) copy-start(f32[512]{0:T(512)} %param.14) | copy-start | bytes 6148
  849.2 10.7 %copy-start.4 = (f32[64]{0:T(128)S(1)}, f32[64]{0:T(128)}, u32[]{:S(2)}) copy-start(f32[64]{0:T(128)} %param.13) | copy-start | bytes 772
  851.3 21.2 %all-to-all-start.3 = ((bf16[32,1,8,512]{3,2,1,0:T(8,128)(2,1)}), bf16[32,1,8,512]{3,2,1,0:T(8,128)(2,1)S(1)}, u32[]{:S(2)}, u32[]{:S(2)}) async-start(bf16[32,1,8,512]{3,2,1,0:T(8,128)(2,1)} %copy.45), calls=%async_computation.3 | async-start | bytes 524288 | tf_op jit(solution)/shard_map/all_to_all | solution.py:106
  860.7 11.8 %copy-start.5 = (bf16[256,512]{1,0:T(8,128)(2,1)S(1)}, bf16[256,512]{1,0:T(8,128)(2,1)}, u32[]{:S(2)}) copy-start(bf16[256,512]{1,0:T(8,128)(2,1)} %param.9) | copy-start | bytes 786436
Sparse Core Ops, SparseCore 0:
  9.5 770.3 all-gather.6
  781.9 45.5 all-gather.4
where the time goes:
time: 884 us
  waiting for transfers between devices  773 us (87%)
  starting transfers between devices  34.8 us (4%)
  blocking collectives  26.3 us (3%)
  local copies, waits for them, and re-layouts  21.9 us (2%)
  between operations  13.6 us (2%)
  matrix products  10.1 us (1%)
    all_gather x1, waiting for transfers between devices, per_device(): factor = lax.all_gather(thc_factor, ROW_COL, axis=1, tiled=True)  742 us
    all_to_all x1, waiting for transfers between devices, exchange_both(): lax.all_to_all(pieces, axis, split_axis=0, concat_axis=0, tiled=True)  20.9 us
  transfers between devices with their start and end apart: 5, of which 3 were waited for; matrix products, arithmetic and copies ran while one was open for 3% of the time, Pallas kernels for 0%

commit v1 on v0

--- a/solution.py
+++ b/solution.py
@@ -69,7 +69,10 @@
     pairs_all = pair_owner.shape[0]
     pairs_col = pairs_all // col_count
     occupied = occ_energy.shape[0]
-    factor = lax.all_gather(thc_factor, ROW_COL, axis=1, tiled=True)
+    n_dev = lax.axis_size(ROW_COL)
+    parts = jnp.stack([thc_factor for _ in range(n_dev)])
+    parts = lax.all_to_all(parts, ROW_COL, split_axis=0, concat_axis=0)
+    factor = jnp.concatenate(parts, axis=1)
     points = factor.shape[1]
     block_points = points // row_count
     core_block = gather_directly(thc_core, "col", 0)

time: 884 us -> 181 us (0.20)
  waiting for transfers between devices: 773 us -> 47.5 us
  starting transfers between devices: 34.8 us -> 55.3 us
    all_gather x1 -> x0, waiting for transfers between devices: 742 us -> none  [per_device(): factor = lax.all_gather(thc_factor, ROW_COL, axis=1, tiled=True)]
    all_to_all x0 -> x2, starting transfers between devices: none -> 25.8 us  [the longest x1 22.1 us: per_device(): parts = lax.all_to_all(parts, ROW_COL, split_axis=0, concat_axis=0)]
    all_to_all x0 -> x2, waiting for transfers between devices: none -> 18.9 us  [the longest x1 12.5 us: per_device(): lax.all_to_all(sectioned_back, ROW, split_axis=1, concat_axis=3, tiled=True)]
    all_to_all x1 -> x0, blocking collectives: 15.6 us -> none  [per_device(): lax.all_to_all(sectioned_back, ROW, split_axis=1, concat_axis=3, tiled=True)]
    all_gather x1, blocking collectives: 10.7 us -> 25.4 us  [gather_in_order(): pieces = lax.all_gather(pieces, axes[k], axis=0, tiled=True)]
    all_to_all x1, starting transfers between devices: 14.5 us -> 4.96 us  [sent_to_all(): lax.all_to_all(jnp.broadcast_to(shard[None], (count, *shard.shape)), axis...]
  transfers between devices with their start and end apart: 5 -> 6, of which waited for: 3 -> 5; matrix products, arithmetic and copies ran while one was open for 3% -> 18% of each run, Pallas kernels for 0% -> 0%
where the time goes in v1:
time: 181 us; the launch traced here: 180 us
  starting transfers between devices  55.3 us (31%)
  waiting for transfers between devices  47.5 us (26%)
  blocking collectives  25.4 us (14%)
  local copies, waits for them, and re-layouts  25.1 us (14%)
  between operations  13.6 us (8%)
  matrix products  10.1 us (6%)
  other arithmetic  2.96 us (2%)
    all_gather x1, blocking collectives, gather_in_order(): pieces = lax.all_gather(pieces, axes[k], axis=0, tiled=True)  25.4 us
    all_to_all x1, starting transfers between devices, per_device(): parts = lax.all_to_all(parts, ROW_COL, split_axis=0, concat_axis=0)  22.1 us
    all_to_all x1, starting transfers between devices, exchange_both(): lax.all_to_all(pieces, axis, split_axis=0, concat_axis=0, tiled=True)  16.6 us
    all_to_all x1, waiting for transfers between devices, exchange_both(): lax.all_to_all(pieces, axis, split_axis=0, concat_axis=0, tiled=True)  16.6 us
    all_to_all x1, waiting for transfers between devices, per_device(): lax.all_to_all(sectioned_back, ROW, split_axis=1, concat_axis=3, tiled=True)  12.5 us
    all_to_all x1, waiting for transfers between devices, per_device(): lax.all_to_all(ladder, 'col', split_axis=0, concat_axis=2, tiled=True)  10.1 us
    unnamed x18, local copies, waits for them, and re-layouts  8.65 us
    all_to_all x1, starting transfers between devices, per_device(): lax.all_to_all(ladder, 'col', split_axis=0, concat_axis=2, tiled=True)  7.91 us
  transfers between devices with their start and end apart: 6, of which 5 were waited for; matrix products, arithmetic and copies ran while one was open for 18% of the time, Pallas kernels for 0%

profile of v1, /device:TPU:1, one launch (start us, length us, event | category | flops | bytes accessed | tf_op | source)
XLA Modules:
  0.0 179.9 jit_solution(14006782499568503142)
XLA Ops:
  6.5 0.0 copy-start
  6.5 0.0 copy-start.1
  6.5 2.2 %stack.2 = bf16[512,512,2]{1,2,0:T(2,128)(2,1)} broadcast(bf16[512,2]{0,1:T(2,128)(2,1)} %param.11), dimensions={1,2} | broadcast | bytes 1050624 | tf_op jit(solution)/shard_map/stack | solution.py:73
  8.8 0.0 copy-start.3
  8.8 22.1 %all-to-all-start.1 = ((bf16[512,512,2]{1,2,0:T(2,128)(2,1)}), bf16[512,512,2]{1,2,0:T(2,128)(2,1)S(1)}, u32[]{:S(2)}, u32[]{:S(2)}) async-start(bf16[512,512,2]{1,2,0:T(2,128)(2,1)} %stack.2), calls=%async_computation.1 | async-start | bytes 2097152 | tf_op jit(solution)/shard_map/all_to_all | solution.py:74
  30.9 0.0 all-gather.3.cloned.1.call-start
  31.0 0.0 copy-done
  31.0 25.4 %all-gather = bf16[32,4096]{1,0:T(8,128)(2,1)} all-gather(bf16[16,4096]{1,0:T(8,128)(2,1)S(1)} %copy-done), channel_id=2, replica_groups=mesh['row_0'=2,'row_1'=8,'col'=32] {'row_0'}, dimensions={0}, use_global_device_ids=true | all-gather | bytes 393216 | tf_op jit(solution)/shard_map/all_gather | solution.py:31
  56.4 0.0 all-gather.3.cloned.1.call-update
  56.4 0.0 copy-done.1
  56.4 0.1 broadcast_in_dim.39
  56.5 1.0 reshape.79
  57.5 6.4 %all-to-all-done.1 = bf16[512,512,2]{1,2,0:T(2,128)(2,1)S(1)} async-done(((bf16[512,512,2]{1,2,0:T(2,128)(2,1)}), bf16[512,512,2]{1,2,0:T(2,128)(2,1)S(1)}, u32[]{:S(2)}, u32[]{:S(2)}) %all-to-all-start.1) | async-done | bytes 1048608 | tf_op jit(solution)/shard_map/all_to_all | solution.py:74
  64.0 5.0 %all-to-all-start = ((f32[32,1,2048]{2,1,0:T(1,128)}), f32[32,1,2048]{2,1,0:T(1,128)}, u32[]{:S(2)}, u32[]{:S(2)}) async-start(f32[32,1,2048]{2,1,0:T(1,128)} %reshape.79), calls=%async_computation | async-start | bytes 524288 | tf_op jit(solution)/shard_map/all_to_all | solution.py:19
  68.9 0.0 copy-done.3
  69.0 3.9 %gather_fusion = bf16[256,512]{1,0:T(8,128)(2,1)S(1)} fusion(bf16[4096,512]{1,0:T(8,128)(2,1)} %param.8, s32[1024]{0:T(1024)S(1)} %pad_clamp_fusion), kind=kCustom, calls=%fused_computation | custom fusion | bytes 525312 | tf_op jit(solution)/shard_map/gather | solution.py:79
  72.9 0.4 reshape.56
  73.4 1.3 convolution_convert_fusion
  74.6 1.8 reshape_reshape.16
  76.4 1.3 copy.48
  77.7 3.0 %reshape.77 = bf16[512,2,256]{2,1,0:T(2,128)(2,1)} reshape(bf16[512,1,1,1,1,1,8,64]{7,6,5,4,3,2,1,0:T(8,128)(2,1)} %bitcast.74) | data formatting | bytes 1048576
  80.6 1.8 %all-to-all-done = f32[32,1,2048]{2,1,0:T(1,128)} async-done(((f32[32,1,2048]{2,1,0:T(1,128)}), f32[32,1,2048]{2,1,0:T(1,128)}, u32[]{:S(2)}, u32[]{:S(2)}) %all-to-all-start) | async-done | bytes 262176 | tf_op jit(solution)/shard_map/all_to_all | solution.py:19
  82.4 16.6 %all-to-all-start.2 = ((bf16[512,2,256]{2,1,0:T(2,128)(2,1)}), bf16[512,2,256]{2,1,0:T(2,128)(2,1)}, u32[]{:S(2)}, u32[]{:S(2)}) async-start(bf16[512,2,256]{2,1,0:T(2,128)(2,1)} %reshape.77), calls=%async_computation.2 | async-start | bytes 1048576 | tf_op jit(solution)/shard_map/all_to_all | solution.py:54
  99.1 0.5 broadcast.22
  99.6 2.2 %reduce.2 = f32[32,2048]{1,0:T(8,128)S(1)} reduce(f32[32,1,2048]{2,1,0:T(1,128)} %all-to-all-done, f32[]{:T(128)} %broadcast.22), dimensions={1}, to_apply=%all_to_all.27.reduce_sub_computation | reduce | bytes 524292 | tf_op jit(solution)/shard_map/all_to_all | solution.py:19
  101.8 0.2 reshape.80
  102.0 0.9 copy.47
  102.9 16.6 %all-to-all-done.2 = bf16[512,2,256]{2,1,0:T(2,128)(2,1)} async-done(((bf16[512,2,256]{2,1,0:T(2,128)(2,1)}), bf16[512,2,256]{2,1,0:T(2,128)(2,1)}, u32[]{:S(2)}, u32[]{:S(2)}) %all-to-all-start.2) | async-done | bytes 524320 | tf_op jit(solution)/shard_map/all_to_all | solution.py:54
  119.5 2.2 %reshape.78 = bf16[512,1,1,1,1,1,8,64]{7,6,5,4,3,2,1,0:T(8,128)(2,1)S(1)} reshape(bf16[512,2,256]{2,1,0:T(2,128)(2,1)} %all-to-all-done.2) | data formatting | bytes 1048576
  121.8 1.0 bitcast_bitcast_fusion
  122.8 3.4 %fusion.1 = bf16[8,512,64]{1,2,0:T(8,128)(2,1)S(1)} fusion(bf16[512,1024]{0,1:T(8,128)(2,1)S(1)} %reshape.56, bf16[8,512,64]{2,0,1:T(8,128)(2,1)} %bitcast_bitcast_fusion, f32[1024,64]{0,1:T(8,128)} %copy.47), kind=kOutput, calls=%fused_computation.6 | convolution fusion | flops 1075052544 | bytes 2359296 | tf_op jit(solution)/shard_map/aP,pPq->paq/dot_general | solution.py:96
  126.2 0.5 copy.54
  126.7 0.1 copy.70
  126.8 1.5 reshape.81
  128.3 3.6 %all-to-all-start.3 = ((bf16[16,2,8192]{2,1,0:T(2,128)(2,1)}), bf16[16,2,8192]{2,1,0:T(2,128)(2,1)S(1)}, u32[]{:S(2)}, u32[]{:S(2)}) async-start(bf16[16,2,8192]{2,1,0:T(2,128)(2,1)} %reshape.81), calls=%async_computation.3 | async-start | bytes 1048576 | tf_op jit(solution)/shard_map/all_to_all | solution.py:101
  131.9 0.4 reshape.75
  132.4 12.5 %all-to-all-done.3 = bf16[16,2,8192]{2,1,0:T(2,128)(2,1)S(1)} async-done(((bf16[16,2,8192]{2,1,0:T(2,128)(2,1)}), bf16[16,2,8192]{2,1,0:T(2,128)(2,1)S(1)}, u32[]{:S(2)}, u32[]{:S(2)}) %all-to-all-start.3) | async-done | bytes 524320 | tf_op jit(solution)/shard_map/all_to_all | solution.py:101
  144.8 0.7 reshape.82
  145.5 0.0 copy-start.2
  145.5 0.0 copy-start.4
  145.5 1.2 convert_reduce_fusion
  146.7 0.9 copy.56
  147.6 7.9 %all-to-all-start.4 = ((bf16[32,1,8,512]{3,2,1,0:T(8,128)(2,1)}), bf16[32,1,8,512]{3,2,1,0:T(8,128)(2,1)S(1)}, u32[]{:S(2)}, u32[]{:S(2)}) async-start(bf16[32,1,8,512]{3,2,1,0:T(8,128)(2,1)} %copy.56), calls=%async_computation.4 | async-start | bytes 524288 | tf_op jit(solution)/shard_map/all_to_all | solution.py:109
  155.5 0.0 copy-done.2
  155.5 0.6 dynamic_slice.3
  156.2 0.0 copy-done.4
  156.2 0.1 select_reduce_fusion
  156.3 0.6 broadcast_add_fusion
  156.9 0.0 all-gather.3.cloned.1.call-done
  156.9 0.0 copy-start.5
  157.0 1.8 copy.46
  158.7 10.1 %all-to-all-done.4 = bf16[32,1,8,512]{3,2,1,0:T(8,128)(2,1)S(1)} async-done(((bf16[32,1,8,512]{3,2,1,0:T(8,128)(2,1)}), bf16[32,1,8,512]{3,2,1,0:T(8,128)(2,1)S(1)}, u32[]{:S(2)}, u32[]{:S(2)}) %all-to-all-start.4) | async-done | bytes 262176 | tf_op jit(solution)/shard_map/all_to_all | solution.py:109
  168.8 0.0 copy-done.5
  168.8 4.2 %fusion.6 = bf16[256,512]{1,0:T(8,128)(2,1)} fusion(bf16[256,4096]{1,0:T(8,128)(2,1)S(1)} %bitcast.79, bf16[4096,512]{1,0:T(8,128)(2,1)} %param.8, bf16[256,512]{1,0:T(8,128)(2,1)S(1)} %copy-done.5, bf16[256,512]{1,0:T(8,128)(2,1)S(1)} %gather_fusion, bf16[32,1,8,512]{3,2,1,0:T(8,128)(2,1)S(1)} %all-to-all-done.4, f32[256]{0:T(256)S(1)} %add.60, ...), kind=kOutput, calls=%fused_computation.12 | convolution fusion | flops 1075183616 | bytes 7343104 | tf_op jit(solution)/shard_map/dot_general | solution.py:80
  (3 shorter events, 0.0 us)
Async XLA Ops:
  6.5 24.5 %copy-start = (bf16[16,4096]{1,0:T(8,128)(2,1)S(1)}, bf16[16,4096]{1,0:T(8,128)(2,1)}, u32[]{:S(2)}) copy-start(bf16[16,4096]{1,0:T(8,128)(2,1)} %param.10) | copy-start | bytes 393220
  6.5 49.9 %copy-start.1 = (f32[32,64]{1,0:T(8,128)S(1)}, f32[32,64]{1,0:T(8,128)}, u32[]{:S(2)}) copy-start(f32[32,64]{1,0:T(8,128)} %param.12) | copy-start | bytes 24580
  8.8 60.2 %copy-start.3 = (s32[256]{0:T(256)S(1)}, s32[256]{0:T(256)}, u32[]{:S(2)}) copy-start(s32[256]{0:T(256)} %param.15) | copy-start | bytes 3076
  8.8 55.2 %all-to-all-start.1 = ((bf16[512,512,2]{1,2,0:T(2,128)(2,1)}), bf16[512,512,2]{1,2,0:T(2,128)(2,1)S(1)}, u32[]{:S(2)}, u32[]{:S(2)}) async-start(bf16[512,512,2]{1,2,0:T(2,128)(2,1)} %stack.2), calls=%async_computation.1 | async-start | bytes 2097152 | tf_op jit(solution)/shard_map/all_to_all | solution.py:74
  30.9 126.0 %all-gather.3.cloned.1.call-start = ((), (), s32[]{:S(2)}) async-start(), calls=%async_computation.5 | async-start | bytes 2359296 | tf_op jit(solution)/shard_map/all_gather | solution.py:31
  64.0 18.5 %all-to-all-start = ((f32[32,1,2048]{2,1,0:T(1,128)}), f32[32,1,2048]{2,1,0:T(1,128)}, u32[]{:S(2)}, u32[]{:S(2)}) async-start(f32[32,1,2048]{2,1,0:T(1,128)} %reshape.79), calls=%async_computation | async-start | bytes 524288 | tf_op jit(solution)/shard_map/all_to_all | solution.py:19
  82.4 37.1 %all-to-all-start.2 = ((bf16[512,2,256]{2,1,0:T(2,128)(2,1)}), bf16[512,2,256]{2,1,0:T(2,128)(2,1)}, u32[]{:S(2)}, u32[]{:S(2)}) async-start(bf16[512,2,256]{2,1,0:T(2,128)(2,1)} %reshape.77), calls=%async_computation.2 | async-start | bytes 1048576 | tf_op jit(solution)/shard_map/all_to_all | solution.py:54
  128.3 16.5 %all-to-all-start.3 = ((bf16[16,2,8192]{2,1,0:T(2,128)(2,1)}), bf16[16,2,8192]{2,1,0:T(2,128)(2,1)S(1)}, u32[]{:S(2)}, u32[]{:S(2)}) async-start(bf16[16,2,8192]{2,1,0:T(2,128)(2,1)} %reshape.81), calls=%async_computation.3 | async-start | bytes 1048576 | tf_op jit(solution)/shard_map/all_to_all | solution.py:101
  145.5 10.0 %copy-start.2 = (f32[512]{0:T(512)S(1)}, f32[512]{0:T(512)}, u32[]{:S(2)}) copy-start(f32[512]{0:T(512)} %param.14) | copy-start | bytes 6148
  145.5 10.7 %copy-start.4 = (f32[64]{0:T(128)S(1)}, f32[64]{0:T(128)}, u32[]{:S(2)}) copy-start(f32[64]{0:T(128)} %param.13) | copy-start | bytes 772
  147.6 21.2 %all-to-all-start.4 = ((bf16[32,1,8,512]{3,2,1,0:T(8,128)(2,1)}), bf16[32,1,8,512]{3,2,1,0:T(8,128)(2,1)S(1)}, u32[]{:S(2)}, u32[]{:S(2)}) async-start(bf16[32,1,8,512]{3,2,1,0:T(8,128)(2,1)} %copy.56), calls=%async_computation.4 | async-start | bytes 524288 | tf_op jit(solution)/shard_map/all_to_all | solution.py:109
  156.9 11.9 %copy-start.5 = (bf16[256,512]{1,0:T(8,128)(2,1)S(1)}, bf16[256,512]{1,0:T(8,128)(2,1)}, u32[]{:S(2)}) copy-start(bf16[256,512]{1,0:T(8,128)(2,1)} %param.9) | copy-start | bytes 786436
Sparse Core Ops, SparseCore 0:
  56.6 40.8 all-gather.2
